TPU v7x, 32 devices: a whole 2x2x4 slice. The times are simulated.
32 devices in a mesh: dp: 8 (over z, y), tensor: 4 (over x, core).
Axes of the slice: x: 2, y: 2, z: 4, core: 2. Of those that a mesh axis runs over, the one named last changes fastest.
Arguments:
- inputs: float32 [1024, 16, 512], P('tensor', 'dp'), may hold values from -6 to 6
- qkv_weight: bfloat16 [3, 512, 512], P(None, 'dp', 'tensor'), may hold values from -0.375 to 0.375
- out_weight: bfloat16 [512, 512], P('tensor', 'dp'), may hold values from -1 to 1
- up_weight: bfloat16 [512, 2048], P('dp', 'tensor'), may hold values from -0.25 to 0.25
- down_weight: bfloat16 [2048, 512], P('tensor', 'dp'), may hold values from -0.125 to 0.125
- gain_one: float32 [512], replicated, may hold values from 0.1 to 1.9
- shift_one: float32 [512], replicated, may hold values from -1.5 to 1.5
- gain_two: float32 [512], replicated, may hold values from 0.1 to 1.9
- shift_two: float32 [512], replicated, may hold values from -1.5 to 1.5
- lengths: int32 [16], P('dp'), may hold values from 512 to 1024, as said below
- teacher: float32 [1024, 16, 512], P('tensor', 'dp'), may hold values from -6 to 6
- cotangent: float32 [1024, 16, 512], P('tensor', 'dp'), may hold values from -6 to 6
Outputs:
- output: float32 [1024, 16, 512], P('tensor', 'dp')
- loss: float32 [], replicated
- grad_inputs: float32 [1024, 16, 512], P('tensor', 'dp')
- grad_qkv: float32 [3, 512, 512], P(None, 'dp', 'tensor')
- grad_out_weight: float32 [512, 512], P('tensor', 'dp')
- grad_up: float32 [512, 2048], P('dp', 'tensor')
- grad_down_weight: float32 [2048, 512], P('tensor', 'dp')
- grad_gain_one: float32 [512], replicated
- grad_shift_one: float32 [512], replicated
- grad_gain_two: float32 [512], replicated
- grad_shift_two: float32 [512], replicated
Inputs may be any that keep to these rules, and one draw needn't show every extreme that they name: `lengths`: some sequence has exactly 1024 valid tokens and some has exactly 512.
All inputs are finite; a program needn't handle non-finite values.
Results may differ from a plain program's by a relative error of at most 0.006.
The roundings to bfloat16 on the way count: a program that leaves them out, or rounds other values in their place, can miss the bound.
Values may be sent and summed in bfloat16 or wider, within the bound.
A program may use at most 128 MiB of HBM per device.

v0:
```python
from functools import partial
import math
import jax
import jax.numpy as jnp
from jax import lax
from jax.sharding import PartitionSpec as P

HD = 64


def norm_rows(values, gain, shift):
    center = values - jnp.mean(values, -1, keepdims=True)
    spread = jnp.mean(center * center, -1, keepdims=True)
    return center * lax.rsqrt(spread + 1e-05) * gain + shift


def angle_tables(positions, width):
    half = width // 2
    rates = jnp.exp(jnp.arange(half, dtype=jnp.float32) * (-2.0 * math.log(10000.0) / width))
    angles = positions.astype(jnp.float32)[:, None] * rates[None, :]
    cosine = jnp.concatenate([jnp.cos(angles), jnp.cos(angles)], -1)[:, None, None, :]
    sine = jnp.concatenate([jnp.sin(angles), jnp.sin(angles)], -1)[:, None, None, :]
    return (cosine, sine)


def turn_half(values):
    half = values.shape[-1] // 2
    return jnp.concatenate([-values[..., half:], values[..., :half]], -1)


def rotate(values, cosine, sine):
    return values * cosine + turn_half(values) * sine


def rotate_back(grads, cosine, sine):
    return grads * cosine - turn_half(grads * sine)


def shards(
    inputs,
    qkv_weight,
    out_weight,
    up_weight,
    down_weight,
    gain_one,
    shift_one,
    gain_two,
    shift_two,
    lengths,
    teacher,
    cotangent,
):
    tensor_size = lax.axis_size("tensor")
    own_rows, sequences, width = inputs.shape
    full_rows = own_rows * tensor_size
    local_width = qkv_weight.shape[2]
    local_heads = local_width // HD
    scale = HD ** (-0.5)
    block_rows = min(512, full_rows)
    starts = list(range(0, full_rows, block_rows))
    total = lax.psum(jnp.sum(lengths).astype(jnp.float32), "dp")
    positions = jnp.arange(full_rows)
    cosine, sine = angle_tables(positions, HD)
    own_positions = lax.axis_index("tensor") * own_rows + jnp.arange(own_rows)
    valid = (own_positions[:, None] < lengths[None, :]).astype(jnp.float32)[:, :, None]

    def allowed_for(start_row):
        query_pos = start_row + jnp.arange(block_rows)
        causal = positions[None, None, None, :] <= query_pos[None, None, :, None]
        return causal & (positions[None, None, None, :] < lengths[:, None, None, None])

    qkv_full, out_full = (
        lax.all_gather(qkv_weight, "dp", axis=1, tiled=True),
        lax.all_gather(out_weight, "dp", axis=1, tiled=True),
    )
    normed = norm_rows(inputs, gain_one, shift_one).astype(jnp.bfloat16)
    normed_all = lax.all_gather(normed, "tensor", axis=0, tiled=True)
    projected = jnp.einsum(
        "lsd,cdk->clsk", normed_all, qkv_full, preferred_element_type=jnp.float32
    )
    shaped = projected.reshape(3, full_rows, sequences, local_heads, HD)
    queries = rotate(shaped[0], cosine, sine).astype(jnp.bfloat16)
    keys_all = rotate(shaped[1], cosine, sine).astype(jnp.bfloat16)
    values_all = shaped[2].astype(jnp.bfloat16)

    def block_scores(start_row):
        block_queries = queries[start_row : start_row + block_rows]
        raw = jnp.einsum(
            "qshe,kshe->shqk", block_queries, keys_all, preferred_element_type=jnp.float32
        )
        return jnp.where(allowed_for(start_row), raw * scale, -1e30)

    mixed_blocks = []
    log_sums = []
    for start_row in starts:
        scores = block_scores(start_row)
        highest = jnp.max(scores, -1, keepdims=True)
        expd = jnp.exp(scores - highest)
        denom = jnp.sum(expd, -1, keepdims=True)
        probs = expd / denom
        log_sums.append(highest + jnp.log(denom))
        mixed_blocks.append(
            jnp.einsum(
                "shqk,kshe->qshe",
                probs.astype(jnp.bfloat16),
                values_all,
                preferred_element_type=jnp.float32,
            )
        )
    attended = (
        jnp.concatenate(mixed_blocks, 0)
        .reshape(full_rows, sequences, local_width)
        .astype(jnp.bfloat16)
    )
    slice_part = attended
    middle_state = inputs + lax.psum_scatter(
        jnp.einsum("lsk,kd->lsd", slice_part, out_full, preferred_element_type=jnp.float32),
        "tensor",
        scatter_dimension=0,
        tiled=True,
    )
    up_weight_gathered, down_weight_gathered = (
        lax.all_gather(up_weight, "dp", axis=0, tiled=True),
        lax.all_gather(down_weight, "dp", axis=1, tiled=True),
    )
    second_normed_rows = norm_rows(middle_state, gain_two, shift_two).astype(jnp.bfloat16)
    second_normed_gathered = lax.all_gather(second_normed_rows, "tensor", axis=0, tiled=True)
    activation_input = jnp.einsum(
        "agm,mt->agt",
        second_normed_gathered,
        up_weight_gathered,
        preferred_element_type=jnp.float32,
    )
    hidden_rows = jax.nn.gelu(activation_input, approximate=False).astype(jnp.bfloat16)
    slice_part = hidden_rows
    output = middle_state + lax.psum_scatter(
        jnp.einsum(
            "bzv,vc->bzc", slice_part, down_weight_gathered, preferred_element_type=jnp.float32
        ),
        "tensor",
        scatter_dimension=0,
        tiled=True,
    )
    differ = output - teacher
    square_part = jnp.sum(valid * differ * differ)
    factor = float(full_rows * sequences * lax.axis_size("dp")) / total
    seed = factor * valid * (cotangent + differ)
    unused_value, gelu_back = jax.vjp(partial(jax.nn.gelu, approximate=False), activation_input)
    grad_output_rows = lax.all_gather(seed.astype(jnp.bfloat16), "tensor", axis=0, tiled=True)
    grad_down_weight = jnp.einsum(
        "aoi,aop->ip", hidden_rows, grad_output_rows, preferred_element_type=jnp.float32
    )
    grad_hidden = jnp.einsum(
        "ecb,gb->ecg", grad_output_rows, down_weight_gathered, preferred_element_type=jnp.float32
    )
    grad_activation_input = gelu_back(grad_hidden)[0].astype(jnp.bfloat16)
    grad_up = jnp.einsum(
        "ckr,ckn->rn",
        second_normed_gathered,
        grad_activation_input,
        preferred_element_type=jnp.float32,
    )
    slice_part = grad_activation_input
    grad_normed_two = lax.psum_scatter(
        jnp.einsum(
            "bmq,eq->bme", slice_part, up_weight_gathered, preferred_element_type=jnp.float32
        ),
        "tensor",
        scatter_dimension=0,
        tiled=True,
    )
    unused_norm, norm_back_two = jax.vjp(norm_rows, middle_state, gain_two, shift_two)
    grad_middle_norm, grad_gain_two, grad_shift_two = norm_back_two(grad_normed_two)
    grad_middle = seed + grad_middle_norm
    grad_branch_rows = lax.all_gather(
        grad_middle.astype(jnp.bfloat16), "tensor", axis=0, tiled=True
    )
    grad_out_w = jnp.einsum(
        "lsk,lsd->kd", attended, grad_branch_rows, preferred_element_type=jnp.float32
    )
    grad_attended = jnp.einsum(
        "lsd,kd->lsk", grad_branch_rows, out_full, preferred_element_type=jnp.float32
    )
    grad_attended = grad_attended.astype(jnp.bfloat16).reshape(
        full_rows, sequences, local_heads, HD
    )
    grad_keys = jnp.zeros((full_rows, sequences, local_heads, HD), jnp.float32)
    grad_values = jnp.zeros((full_rows, sequences, local_heads, HD), jnp.float32)
    grad_query_blocks = []
    for block_index, start_row in enumerate(starts):
        scores = block_scores(start_row)
        probs = jnp.exp(scores - log_sums[block_index])
        block_grad = grad_attended[start_row : start_row + block_rows]
        grad_probs = jnp.einsum(
            "qshe,kshe->shqk", block_grad, values_all, preferred_element_type=jnp.float32
        )
        inner = jnp.sum(probs * grad_probs, -1, keepdims=True)
        grad_raw = (probs * (grad_probs - inner) * scale).astype(jnp.bfloat16)
        grad_query_blocks.append(
            jnp.einsum("shqk,kshe->qshe", grad_raw, keys_all, preferred_element_type=jnp.float32)
        )
        grad_keys = grad_keys + jnp.einsum(
            "shqk,qshe->kshe",
            grad_raw,
            queries[start_row : start_row + block_rows],
            preferred_element_type=jnp.float32,
        )
        grad_values = grad_values + jnp.einsum(
            "shqk,qshe->kshe",
            probs.astype(jnp.bfloat16),
            block_grad,
            preferred_element_type=jnp.float32,
        )
    grad_queries = jnp.concatenate(grad_query_blocks, 0)
    grad_projected = jnp.stack(
        [rotate_back(grad_queries, cosine, sine), rotate_back(grad_keys, cosine, sine), grad_values]
    )
    grad_projected = grad_projected.astype(jnp.bfloat16).reshape(
        3, full_rows, sequences, local_width
    )
    grad_qkv = jnp.einsum(
        "lsd,clsk->cdk", normed_all, grad_projected, preferred_element_type=jnp.float32
    )
    slice_part = grad_projected
    grad_normed = lax.psum_scatter(
        jnp.einsum("clsk,cdk->lsd", slice_part, qkv_full, preferred_element_type=jnp.float32),
        "tensor",
        scatter_dimension=0,
        tiled=True,
    )
    unused_first, norm_back_one = jax.vjp(norm_rows, inputs, gain_one, shift_one)
    grad_inputs_norm, grad_gain_one, grad_shift_one = norm_back_one(grad_normed)
    grad_inputs = grad_middle + grad_inputs_norm
    grad_qkv, grad_out_w, grad_up, grad_down_weight = (
        lax.psum_scatter(grad_qkv, "dp", scatter_dimension=1, tiled=True),
        lax.psum_scatter(grad_out_w, "dp", scatter_dimension=1, tiled=True),
        lax.psum_scatter(grad_up, "dp", scatter_dimension=0, tiled=True),
        lax.psum_scatter(grad_down_weight, "dp", scatter_dimension=1, tiled=True),
    )
    square_sum, grad_gain_one, grad_shift_one, grad_gain_two, grad_shift_two = lax.psum(
        (square_part, grad_gain_one, grad_shift_one, grad_gain_two, grad_shift_two),
        ("dp", "tensor"),
    )
    loss = square_sum / (total * width)
    return (
        output,
        loss,
        grad_inputs,
        grad_qkv,
        grad_out_w,
        grad_up,
        grad_down_weight,
        grad_gain_one,
        grad_shift_one,
        grad_gain_two,
        grad_shift_two,
    )


def solution(mesh):
    placed = (
        P("tensor", "dp", None),
        P(None, "dp", "tensor"),
        P("tensor", "dp"),
        P("dp", "tensor"),
        P("tensor", "dp"),
        P(),
        P(),
        P(),
        P(),
        P("dp"),
        P("tensor", "dp", None),
        P("tensor", "dp", None),
    )
    return jax.shard_map(
        shards,
        mesh=mesh,
        in_specs=placed,
        out_specs=(
            P("tensor", "dp", None),
            P(),
            P("tensor", "dp", None),
            P(None, "dp", "tensor"),
            P("tensor", "dp"),
            P("dp", "tensor"),
            P("tensor", "dp"),
            P(),
            P(),
            P(),
            P(),
        ),
        check_vma=False,
    )
```

profile of v0, /device:TPU:0, one launch (start us, length us, event | category | flops | bytes accessed | tf_op | source)
XLA Modules:
  0.0 849.0 jit_solution(6604862089245916614)
XLA Ops:
  13.0 32.3 %all_gather.26 = bf16[128,512]{0,1:T(8,128)(2,1)S(1)} all-gather(bf16[128,64]{0,1:T(8,128)(2,1)S(1)} %copy-done.47), channel_id=1, replica_groups=mesh['dp'=8,'tensor'=4] {'dp'}, dimensions={1}, use_global_device_ids=true | all-gather | bytes 147456 | tf_op jit(solution)/shard_map/all_gather | solution.py:74
  46.8 31.1 %all_gather.25 = bf16[3,512,128]{2,1,0:T(8,128)(2,1)S(1)} all-gather(bf16[3,64,128]{2,1,0:T(8,128)(2,1)S(1)} %copy-done.35), channel_id=1, replica_groups=mesh['dp'=8,'tensor'=4] {'dp'}, dimensions={1}, use_global_device_ids=true | all-gather | bytes 442368 | tf_op jit(solution)/shard_map/all_gather | solution.py:73
  88.5 4.7 fusion.4
  102.9 45.8 %reduce-scatter.8.cloned.1.call-done = f32[256,2,512]{2,0,1:T(8,128)} async-done(((f32[1024,2,512]{2,0,1:T(8,128)}), f32[256,2,512]{2,0,1:T(8,128)}) %reduce-scatter.8.cloned.1.call-update) | async-done | bytes 1048592 | tf_op jit(solution)/shard_map/reduce_scatter | solution.py:116
  151.7 31.6 %all_gather.28 = bf16[512,512]{1,0:T(8,128)(2,1)S(1)} all-gather(bf16[64,512]{1,0:T(8,128)(2,1)S(1)} %copy-done.34), channel_id=1, replica_groups=mesh['dp'=8,'tensor'=4] {'dp'}, dimensions={0}, use_global_device_ids=true | all-gather | bytes 589824 | tf_op jit(solution)/shard_map/all_gather | solution.py:123
  183.3 31.6 %all_gather.29 = bf16[512,512]{0,1:T(8,128)(2,1)S(1)} all-gather(bf16[512,64]{0,1:T(8,128)(2,1)} %param.16), channel_id=1, replica_groups=mesh['dp'=8,'tensor'=4] {'dp'}, dimensions={1}, use_global_device_ids=true | all-gather | bytes 589824 | tf_op jit(solution)/shard_map/all_gather | solution.py:124
  214.9 4.5 fusion.108
  219.4 10.7 %multiply_convert_fusion.2 = (bf16[1024,2,512]{2,0,1:T(8,128)(2,1)S(1)}, f32[1024,2,512]{2,0,1:T(8,128)}) fusion(f32[1024,2,512]{2,0,1:T(8,128)S(1)} %get-tuple-element.113, u8[1024,512]{1,0:T(8,128)(4,1)S(1)} %get-tuple-element.67, u8[1024,512]{1,0:T(8,128)(4,1)S(1)} %get-tuple-element.66), kind=kLoop, calls=%fused_computation.38 | loop fusion | flops 73400320 | bytes 11534336 | tf_op jit(solution)/shard_map/convert_element_type | solution.py:134
  236.1 21.9 %psum.43 = f32[]{:T(128)} all-reduce(f32[]{:T(128)S(6)} %convert_element_type.90), channel_id=1, replica_groups=mesh['dp'=8,'tensor'=4] {'dp'}, use_global_device_ids=true, to_apply=%region_13.14 | all-reduce | flops 1 | bytes 8 | tf_op jit(solution)/shard_map/psum | solution.py:61
  259.4 20.1 %reduce-scatter.10.cloned.1.call-done = f32[256,2,512]{2,0,1:T(8,128)} async-done(((f32[1024,2,512]{2,0,1:T(8,128)}), f32[256,2,512]{2,0,1:T(8,128)}) %reduce-scatter.10.cloned.1.call-update) | async-done | bytes 1048592 | tf_op jit(solution)/shard_map/reduce_scatter | solution.py:136
  279.6 3.5 fusion.164
  283.1 22.7 %all-gather.9.cloned.1.call-done = bf16[1024,2,512]{2,0,1:T(8,128)(2,1)} async-done(((bf16[256,2,512]{2,0,1:T(8,128)(2,1)}), bf16[1024,2,512]{2,0,1:T(8,128)(2,1)}) %all-gather.9.cloned.1.call-update) | async-done | bytes 2097168 | tf_op jit(solution)/shard_map/all_gather | solution.py:149
  305.8 6.7 add_convert_fusion
  317.1 44.7 %reduce-scatter.12.cloned.1.call-done = f32[256,2,512]{2,0,1:T(8,128)} async-done(((f32[1024,2,512]{2,0,1:T(8,128)}), f32[256,2,512]{2,0,1:T(8,128)}) %reduce-scatter.12.cloned.1.call-update) | async-done | bytes 1048592 | tf_op jit(solution)/shard_map/reduce_scatter | solution.py:164
  372.2 19.0 %all-gather.11.cloned.1.call-done = bf16[1024,2,512]{2,0,1:T(8,128)(2,1)} async-done(((bf16[256,2,512]{2,0,1:T(8,128)(2,1)}), bf16[1024,2,512]{2,0,1:T(8,128)(2,1)}) %all-gather.11.cloned.1.call-update) | async-done | bytes 2097168 | tf_op jit(solution)/shard_map/all_gather | solution.py:175
  395.1 4.5 fusion.172
  399.6 23.6 %fusion.17 = f32[2,2,64,512]{3,2,1,0:T(8,128)} fusion(bf16[1024,2,2,64]{0,3,2,1:T(8,128)(2,1)S(1)} %copy-done.33, f32[2,2,512,1024]{3,2,1,0:T(8,128)} %fusion.172, f32[2,2,512,1024]{3,2,1,0:T(8,128)} %copy-done.6, f32[2,2,512]{2,1,0:T(2,128)S(1)} %copy-done.49, pred[2,512,1024]{2,1,0:T(8,128)(4,1)} %copy-done.16), kind=kOutput, calls=%fused_computation.23 | convolution fusion | flops 291507200 | bytes 18882560 | tf_op jit(solution)/shard_map/shqk,kshe->qshe/dot_general | solution.py:200
  423.2 19.1 %fusion.14 = f32[2,2,64,1024]{3,2,1,0:T(8,128)} fusion(f32[2,2,512,1024]{3,2,1,0:T(8,128)} %fusion.172, f32[2,2,512,1024]{3,2,1,0:T(8,128)} %copy-done.6, f32[2,2,512]{2,1,0:T(2,128)S(1)} %copy-done.49, pred[2,512,1024]{2,1,0:T(8,128)(4,1)} %copy-done.16, bf16[1024,2,2,64]{0,3,2,1:T(8,128)(2,1)} %copy-done.31), kind=kOutput, calls=%fused_computation.22 | convolution fusion | flops 291507200 | bytes 36978688 | tf_op jit(solution)/shard_map/shqk,qshe->kshe/dot_general | solution.py:202
  442.4 4.5 fusion.173
  446.9 5.0 fusion.56
  452.0 3.5 fusion.91
  458.5 18.4 %fusion.24 = f32[2,2,64,512]{3,2,1,0:T(8,128)} fusion(bf16[1024,2,2,64]{0,3,2,1:T(8,128)(2,1)} %copy-done.32, f32[2,2,512,1024]{3,2,1,0:T(8,128)} %fusion.173, f32[2,2,512,1024]{3,2,1,0:T(8,128)} %copy-done.5, f32[2,2,512]{2,1,0:T(2,128)S(1)} %copy-done.48, pred[2,512,1024]{2,1,0:T(8,128)(4,1)} %copy-done.14), kind=kOutput, calls=%fused_computation.26 | convolution fusion | flops 291507200 | bytes 18882560 | tf_op jit(solution)/shard_map/shqk,kshe->qshe/dot_general | solution.py:200
  476.9 20.5 %maximum_multiply_fusion.3 = (f32[1024,2,2,64]{0,3,2,1:T(8,128)}, f32[1024,2,2,64]{0,3,2,1:T(8,128)}, f32[1024,2,2,64]{0,3,2,1:T(8,128)}) fusion(f32[512,2,2,64]{0,3,2,1:T(8,128)} %bitcast.122, f32[512,2,2,64]{0,3,2,1:T(8,128)S(1)} %bitcast.121, f32[1024,64]{0,1:T(8,128)S(1)} %copy-done.25, f32[2,2,64,1024]{3,2,1,0:T(8,128)} %fusion.14, ...), kind=kOutput, calls=%fused_computation.107 | convolution fusion | flops 292555776 | bytes 41435136 | tf_op jit(solution)/shard_map/shqk,qshe->kshe/dot_general | solution.py:202
  515.6 4.6 convolution_bitcast_fusion
  520.3 4.7 convolution_bitcast_fusion.2
  525.3 4.5 convolution_bitcast_fusion.1
  537.7 56.4 %all-reduce.4.cloned.1.call-done = f32[3,512,128]{2,0,1:T(4,128)} async-done(((f32[3,512,128]{2,0,1:T(4,128)}), f32[3,512,128]{2,0,1:T(4,128)}) %all-reduce.4.cloned.1.call-update) | async-done | bytes 786448
  595.6 45.1 %reduce-scatter.14.cloned.1.call-done = f32[256,2,512]{2,0,1:T(8,128)} async-done(((f32[1024,2,512]{2,0,1:T(8,128)}), f32[256,2,512]{2,0,1:T(8,128)}) %reduce-scatter.14.cloned.1.call-update) | async-done | bytes 1048592 | tf_op jit(solution)/shard_map/reduce_scatter | solution.py:225
  644.4 40.0 %all-reduce.1 = (f32[]{:T(128)}, f32[512]{0:T(512)}, f32[512]{0:T(512)}, f32[512]{0:T(512)}, f32[512]{0:T(512)}) all-reduce(f32[]{:T(128)} %fusion.98, f32[512]{0:T(512)S(1)} %get-tuple-element.68, f32[512]{0:T(512)S(1)} %get-tuple-element.73, f32[512]{0:T(512)S(1)} %copy-done.50, ...), channel_id=1, replica_groups=mesh['dp'=8,'tensor'=4] {'dp','tensor'}, use_global_device_ids=true, to_apply=%region_11.12 | all-reduce | flops 2049 | bytes 16392 | tf_op jit(solution)/shard_map/psum | solution.py:240
  688.6 20.3 %reduce-scatter.18.cloned.1.call-done = f32[64,512]{1,0:T(8,128)} async-done(((f32[512,512]{1,0:T(8,128)}), f32[64,512]{1,0:T(8,128)}) %reduce-scatter.18.cloned.1.call-update) | async-done | bytes 131088 | tf_op jit(solution)/shard_map/reduce_scatter | solution.py:237
  708.9 67.1 %reduce-scatter.20.cloned.1.call-done = f32[512,64]{0,1:T(8,128)} async-done(((f32[512,512]{0,1:T(8,128)}), f32[512,64]{0,1:T(8,128)}) %reduce-scatter.20.cloned.1.call-update) | async-done | bytes 131088 | tf_op jit(solution)/shard_map/reduce_scatter | solution.py:238
  776.0 64.8 %reduce-scatter.16.cloned.1.call-done = f32[128,64]{0,1:T(8,128)} async-done(((f32[128,512]{0,1:T(8,128)}), f32[128,64]{0,1:T(8,128)}) %reduce-scatter.16.cloned.1.call-update) | async-done | bytes 32784 | tf_op jit(solution)/shard_map/reduce_scatter | solution.py:236
  (223 shorter events, 91.7 us)
Async XLA Ops:
  7.2 39.6 %copy-start.35 = (bf16[3,64,128]{2,1,0:T(8,128)(2,1)S(1)}, bf16[3,64,128]{2,1,0:T(8,128)(2,1)}, u32[]{:S(2)}) copy-start(bf16[3,64,128]{2,1,0:T(8,128)(2,1)} %param.13) | copy-start | bytes 147460
  7.2 70.7 %copy-start.52 = (s32[2]{0:T(128)S(1)}, s32[2]{0:T(128)}, u32[]{:S(2)}) copy-start(s32[2]{0:T(128)} %param.21) | copy-start | bytes 28
  7.2 72.2 %all-gather.5.cloned.1.call-start = ((), (), s32[]{:S(2)}) async-start(), calls=%async_computation.7 | async-start | bytes 2621440 | tf_op jit(solution)/shard_map/all_gather | solution.py:77
  10.5 72.2 %copy-start.43 = (f32[256,2]{0,1:T(2,128)}, f32[256,2]{0,1:T(2,128)S(1)}, u32[]{:S(2)}) copy-start(f32[256,2]{0,1:T(2,128)S(1)} %multiply_reduce_fusion.7) | copy-start | bytes 6148
  10.5 72.2 %copy-start.39 = (f32[256,2]{0,1:T(2,128)}, f32[256,2]{0,1:T(2,128)S(1)}, u32[]{:S(2)}) copy-start(f32[256,2]{0,1:T(2,128)S(1)} %fusion.130) | copy-start | bytes 6148
  12.9 135.8 %reduce-scatter.8.cloned.1.call-start = ((), (), s32[]{:S(2)}) async-start(), calls=%async_computation.8 | async-start | bytes 5242880 | tf_op jit(solution)/shard_map/reduce_scatter | solution.py:116
  79.3 16.9 %copy-start.16 = (pred[2,512,1024]{2,1,0:T(8,128)(4,1)}, pred[2,512,1024]{2,1,0:T(8,128)(4,1)S(1)}, u32[]{:S(2)}) copy-start(pred[2,512,1024]{2,1,0:T(8,128)(4,1)S(1)} %get-tuple-element.107) | copy-start | bytes 3145732
  100.1 48.6 %copy-start = (f32[256,2,512]{2,1,0:T(2,128)S(1)}, f32[256,2,512]{2,1,0:T(2,128)}, u32[]{:S(2)}) copy-start(f32[256,2,512]{2,1,0:T(2,128)} %param.12) | copy-start | bytes 3145732
  102.8 47.7 %copy-start.46 = (f32[512]{0:T(512)S(1)}, f32[512]{0:T(512)}, u32[]{:S(2)}) copy-start(f32[512]{0:T(512)} %param.19) | copy-start | bytes 6148
  102.8 47.7 %copy-start.57 = (f32[512]{0:T(512)S(1)}, f32[512]{0:T(512)}, u32[]{:S(2)}) copy-start(f32[512]{0:T(512)} %param.20) | copy-start | bytes 6148
  102.8 48.8 %copy-start.34 = (bf16[64,512]{1,0:T(8,128)(2,1)S(1)}, bf16[64,512]{1,0:T(8,128)(2,1)}, u32[]{:S(2)}) copy-start(bf16[64,512]{1,0:T(8,128)(2,1)} %param.15) | copy-start | bytes 196612
  102.8 112.0 %all-gather.7.cloned.1.call-start = ((), (), s32[]{:S(2)}) async-start(), calls=%async_computation.9 | async-start | bytes 2621440 | tf_op jit(solution)/shard_map/all_gather | solution.py:127
  151.6 128.0 %reduce-scatter.10.cloned.1.call-start = ((), (), s32[]{:S(2)}) async-start(), calls=%async_computation.10 | async-start | bytes 5242880 | tf_op jit(solution)/shard_map/reduce_scatter | solution.py:136
  183.3 36.1 %copy-start.21 = (bf16[512,512]{1,0:T(8,128)(2,1)}, bf16[512,512]{1,0:T(8,128)(2,1)S(1)}, u32[]{:S(2)}) copy-start(bf16[512,512]{1,0:T(8,128)(2,1)S(1)} %all_gather.28) | copy-start | bytes 1572868
  234.8 71.0 %all-gather.9.cloned.1.call-start = ((), (), s32[]{:S(2)}) async-start(), calls=%async_computation.11 | async-start | bytes 2621440 | tf_op jit(solution)/shard_map/all_gather | solution.py:149
  283.1 78.7 %reduce-scatter.12.cloned.1.call-start = ((), (), s32[]{:S(2)}) async-start(), calls=%async_computation.12 | async-start | bytes 5242880 | tf_op jit(solution)/shard_map/reduce_scatter | solution.py:164
  317.1 74.1 %all-gather.11.cloned.1.call-start = ((), (), s32[]{:S(2)}) async-start(), calls=%async_computation.13 | async-start | bytes 2621440 | tf_op jit(solution)/shard_map/all_gather | solution.py:175
  367.5 27.6 %copy-start.11 = (bf16[1,1024,2,128]{1,3,0,2:T(8,128)(2,1)S(1)}, bf16[1,1024,2,128]{1,3,0,2:T(8,128)(2,1)}, u32[]{:S(2)}) copy-start(bf16[1,1024,2,128]{1,3,0,2:T(8,128)(2,1)} %copy-done.10) | copy-start | bytes 1572868
  368.5 225.6 %all-reduce.4.cloned.1.call-start = ((), (), s32[]{:S(2)}) async-start(), calls=%async_computation.18 | async-start | bytes 2097152
  423.2 19.2 %copy-start.28 = (bf16[512,2,128]{0,2,1:T(8,128)(2,1)S(1)}, bf16[512,2,128]{0,2,1:T(8,128)(2,1)}, u32[]{:S(2)}) copy-start(bf16[512,2,128]{0,2,1:T(8,128)(2,1)} %get-tuple-element.100) | copy-start | bytes 786436
  458.5 18.4 %copy-start.25 = (f32[1024,64]{0,1:T(8,128)S(1)}, f32[1024,64]{0,1:T(8,128)}, u32[]{:S(2)}) copy-start(f32[1024,64]{0,1:T(8,128)} %pad_maximum_fusion.6) | copy-start | bytes 786436
  515.6 125.2 %reduce-scatter.14.cloned.1.call-start = ((), (), s32[]{:S(2)}) async-start(), calls=%async_computation.14 | async-start | bytes 5242880 | tf_op jit(solution)/shard_map/reduce_scatter | solution.py:225
  520.3 188.6 %reduce-scatter.18.cloned.1.call-start = ((), (), s32[]{:S(2)}) async-start(), calls=%async_computation.16 | async-start | bytes 1179648 | tf_op jit(solution)/shard_map/reduce_scatter | solution.py:237
  525.0 251.0 %reduce-scatter.20.cloned.1.call-start = ((), (), s32[]{:S(2)}) async-start(), calls=%async_computation.17 | async-start | bytes 1179648 | tf_op jit(solution)/shard_map/reduce_scatter | solution.py:238
  529.9 110.9 %copy-start.41 = (f32[512]{0:T(512)S(1)}, f32[512]{0:T(512)}, u32[]{:S(2)}) copy-start(f32[512]{0:T(512)} %param.17) | copy-start | bytes 6148
  529.9 310.9 %reduce-scatter.16.cloned.1.call-start = ((), (), s32[]{:S(2)}) async-start(), calls=%async_computation.15 | async-start | bytes 294912 | tf_op jit(solution)/shard_map/reduce_scatter | solution.py:236
  533.7 108.7 %copy-start.44 = (f32[256,2]{0,1:T(2,128)S(1)}, f32[256,2]{0,1:T(2,128)}, u32[]{:S(2)}) copy-start(f32[256,2]{0,1:T(2,128)} %copy-done.43) | copy-start | bytes 6148
  533.7 108.8 %copy-start.40 = (f32[256,2]{0,1:T(2,128)S(1)}, f32[256,2]{0,1:T(2,128)}, u32[]{:S(2)}) copy-start(f32[256,2]{0,1:T(2,128)} %copy-done.39) | copy-start | bytes 6148
  536.0 108.4 %copy-start.50 = (f32[512]{0:T(512)S(1)}, f32[512]{0:T(512)}, u32[]{:S(2)}) copy-start(f32[512]{0:T(512)} %get-tuple-element.70) | copy-start | bytes 6148
  536.0 108.4 %copy-start.51 = (f32[512]{0:T(512)S(1)}, f32[512]{0:T(512)}, u32[]{:S(2)}) copy-start(f32[512]{0:T(512)} %get-tuple-element.72) | copy-start | bytes 6148
  536.0 148.5 %copy-start.2 = (f32[256,2,512]{2,0,1:T(8,128)S(1)}, f32[256,2,512]{2,0,1:T(8,128)}, u32[]{:S(2)}) copy-start(f32[256,2,512]{2,0,1:T(8,128)} %get-tuple-element.83) | copy-start | bytes 3145732
  640.7 43.7 %copy-start.3 = (f32[256,2,512]{2,0,1:T(8,128)S(1)}, f32[256,2,512]{2,0,1:T(8,128)}, u32[]{:S(2)}) copy-start(f32[256,2,512]{2,0,1:T(8,128)} %reduce-scatter.14.cloned.1.call-done) | copy-start | bytes 3145732
  (41 other events, 205.3 us)
Sparse Core Ops, SparseCore 0:
  13.0 25.2 all-gather.4
  103.0 45.6 reduce-scatter.7
  151.7 22.5 all-gather.6
  234.9 44.6 reduce-scatter.9
  283.2 22.5 all-gather.8
  317.2 44.5 reduce-scatter.11
  368.6 22.5 all-gather.10
  515.7 78.2 all-reduce.3
  596.5 44.1 reduce-scatter.13
  644.6 64.2 reduce-scatter.17
  712.9 63.1 reduce-scatter.19
  779.8 60.9 reduce-scatter.15
where the time goes:
time: 853 us; the launch traced here: 849 us
  waiting for transfers between devices  406 us (48%)
  blocking collectives  189 us (22%)
  matrix products  154 us (18%)
  other arithmetic  55.5 us (7%)
  local copies, waits for them, and re-layouts  24.8 us (3%)
  between operations  19.7 us (2%)
    reduce_scatter x1, waiting for transfers between devices, shards(): lax.psum_scatter(grad_down_weight, 'dp', scatter_dimension=1, tiled=True)  67.1 us
    reduce_scatter x1, waiting for transfers between devices, shards(): lax.psum_scatter(grad_out_w, 'dp', scatter_dimension=1, tiled=True)  64.8 us
    unnamed x13, waiting for transfers between devices  56.6 us
    reduce_scatter x1, waiting for transfers between devices, shards(): lax.psum_scatter(jnp.einsum('lsk,kd->lsd', slice_part, out_full, preferre...  45.8 us
    reduce_scatter x1, waiting for transfers between devices, shards(): lax.psum_scatter(jnp.einsum('clsk,cdk->lsd', slice_part, qkv_full, prefer...  45.1 us
    reduce_scatter x1, waiting for transfers between devices, shards(): lax.psum_scatter(jnp.einsum('bmq,eq->bme', slice_part, up_weight_gathered...  44.7 us
    dot_general x2, matrix products, shards(): jnp.einsum('shqk,kshe->qshe', grad_raw, keys_all, preferred_element_type=...  42.1 us
    psum x1, blocking collectives, shards(): lax.psum((square_part, grad_gain_one, grad_shift_one, grad_gain_two, grad...  40 us
  transfers between devices with their start and end apart: 12, of which 10 were waited for; matrix products, arithmetic and copies ran while one was open for 4% of the time, Pallas kernels for 0%

commit v1 on v0

--- a/solution.py
+++ b/solution.py
@@ -58,7 +58,7 @@
     scale = HD ** (-0.5)
     block_rows = min(512, full_rows)
     starts = list(range(0, full_rows, block_rows))
-    total = lax.psum(jnp.sum(lengths).astype(jnp.float32), "dp")
+    total = jnp.sum(lax.all_gather(jnp.sum(lengths).astype(jnp.float32), "dp"), axis=0)
     positions = jnp.arange(full_rows)
     cosine, sine = angle_tables(positions, HD)
     own_positions = lax.axis_index("tensor") * own_rows + jnp.arange(own_rows)

time: 853 us -> 852 us (level)
    psum x1 -> x0, blocking collectives: 21.9 us -> none  [shards(): total = lax.psum(jnp.sum(lengths).astype(jnp.float32), 'dp')]
    unnamed x0 -> x1, blocking collectives: none -> 21.3 us
where the time goes in v1:
time: 852 us; the launch traced here: 849 us
  waiting for transfers between devices  405 us (48%)
  blocking collectives  188 us (22%)
  matrix products  153 us (18%)
  other arithmetic  56.1 us (7%)
  local copies, waits for them, and re-layouts  25.5 us (3%)
  between operations  19.7 us (2%)
    reduce_scatter x1, waiting for transfers between devices, shards(): lax.psum_scatter(grad_down_weight, 'dp', scatter_dimension=1, tiled=True)  67.1 us
    reduce_scatter x1, waiting for transfers between devices, shards(): lax.psum_scatter(grad_out_w, 'dp', scatter_dimension=1, tiled=True)  64.8 us
    unnamed x13, waiting for transfers between devices  57.1 us
    reduce_scatter x1, waiting for transfers between devices, shards(): lax.psum_scatter(jnp.einsum('lsk,kd->lsd', slice_part, out_full, preferre...  45.8 us
    reduce_scatter x1, waiting for transfers between devices, shards(): lax.psum_scatter(jnp.einsum('clsk,cdk->lsd', slice_part, qkv_full, prefer...  45.1 us
    reduce_scatter x1, waiting for transfers between devices, shards(): lax.psum_scatter(jnp.einsum('bmq,eq->bme', slice_part, up_weight_gathered...  44.7 us
    dot_general x2, matrix products, shards(): jnp.einsum('shqk,kshe->qshe', grad_raw, keys_all, preferred_element_type=...  41.7 us
    psum x1, blocking collectives, shards(): lax.psum((square_part, grad_gain_one, grad_shift_one, grad_gain_two, grad...  40 us
  transfers between devices with their start and end apart: 12, of which 10 were waited for; matrix products, arithmetic and copies ran while one was open for 4% of the time, Pallas kernels for 0%

profile of v1, /device:TPU:0, one launch (start us, length us, event | category | flops | bytes accessed | tf_op | source)
XLA Modules:
  0.0 848.6 jit_solution(13265177248675624915)
XLA Ops:
  13.0 32.3 %all_gather.32 = bf16[128,512]{0,1:T(8,128)(2,1)S(1)} all-gather(bf16[128,64]{0,1:T(8,128)(2,1)S(1)} %copy-done.47), channel_id=1, replica_groups=mesh['dp'=8,'tensor'=4] {'dp'}, dimensions={1}, use_global_device_ids=true | all-gather | bytes 147456 | tf_op jit(solution)/shard_map/all_gather | solution.py:74
  46.8 31.1 %all_gather.31 = bf16[3,512,128]{2,1,0:T(8,128)(2,1)S(1)} all-gather(bf16[3,64,128]{2,1,0:T(8,128)(2,1)S(1)} %copy-done.35), channel_id=1, replica_groups=mesh['dp'=8,'tensor'=4] {'dp'}, dimensions={1}, use_global_device_ids=true | all-gather | bytes 442368 | tf_op jit(solution)/shard_map/all_gather | solution.py:73
  88.5 4.7 fusion.4
  102.9 45.8 %reduce-scatter.8.cloned.1.call-done = f32[256,2,512]{2,0,1:T(8,128)} async-done(((f32[1024,2,512]{2,0,1:T(8,128)}), f32[256,2,512]{2,0,1:T(8,128)}) %reduce-scatter.8.cloned.1.call-update) | async-done | bytes 1048592 | tf_op jit(solution)/shard_map/reduce_scatter | solution.py:116
  151.6 31.7 %all_gather.34 = bf16[512,512]{1,0:T(8,128)(2,1)S(1)} all-gather(bf16[64,512]{1,0:T(8,128)(2,1)S(1)} %copy-done.34), channel_id=1, replica_groups=mesh['dp'=8,'tensor'=4] {'dp'}, dimensions={0}, use_global_device_ids=true | all-gather | bytes 589824 | tf_op jit(solution)/shard_map/all_gather | solution.py:123
  183.3 31.6 %all_gather.35 = bf16[512,512]{0,1:T(8,128)(2,1)S(1)} all-gather(bf16[512,64]{0,1:T(8,128)(2,1)} %param.16), channel_id=1, replica_groups=mesh['dp'=8,'tensor'=4] {'dp'}, dimensions={1}, use_global_device_ids=true | all-gather | bytes 589824 | tf_op jit(solution)/shard_map/all_gather | solution.py:124
  214.9 4.5 fusion.108
  219.4 10.7 %multiply_convert_fusion.2 = (bf16[1024,2,512]{2,0,1:T(8,128)(2,1)S(1)}, f32[1024,2,512]{2,0,1:T(8,128)}) fusion(f32[1024,2,512]{2,0,1:T(8,128)S(1)} %get-tuple-element.115, u8[1024,512]{1,0:T(8,128)(4,1)S(1)} %get-tuple-element.67, u8[1024,512]{1,0:T(8,128)(4,1)S(1)} %get-tuple-element.66), kind=kLoop, calls=%fused_computation.38 | loop fusion | flops 73400320 | bytes 11534336 | tf_op jit(solution)/shard_map/convert_element_type | solution.py:134
  237.5 21.3 %all-reduce = f32[8]{0:T(128)S(1)} all-reduce(f32[8]{0:T(128)S(1)} %dynamic-update-slice), channel_id=1, replica_groups=mesh['dp'=8,'tensor'=4] {'dp'}, use_global_device_ids=true, to_apply=%add | all-reduce | flops 8 | bytes 64
  260.8 18.7 %reduce-scatter.10.cloned.1.call-done = f32[256,2,512]{2,0,1:T(8,128)} async-done(((f32[1024,2,512]{2,0,1:T(8,128)}), f32[256,2,512]{2,0,1:T(8,128)}) %reduce-scatter.10.cloned.1.call-update) | async-done | bytes 1048592 | tf_op jit(solution)/shard_map/reduce_scatter | solution.py:136
  279.5 3.5 fusion.164
  283.1 22.7 %all-gather.9.cloned.1.call-done = bf16[1024,2,512]{2,0,1:T(8,128)(2,1)} async-done(((bf16[256,2,512]{2,0,1:T(8,128)(2,1)}), bf16[1024,2,512]{2,0,1:T(8,128)(2,1)}) %all-gather.9.cloned.1.call-update) | async-done | bytes 2097168 | tf_op jit(solution)/shard_map/all_gather | solution.py:149
  305.8 6.7 add_convert_fusion
  317.1 44.7 %reduce-scatter.12.cloned.1.call-done = f32[256,2,512]{2,0,1:T(8,128)} async-done(((f32[1024,2,512]{2,0,1:T(8,128)}), f32[256,2,512]{2,0,1:T(8,128)}) %reduce-scatter.12.cloned.1.call-update) | async-done | bytes 1048592 | tf_op jit(solution)/shard_map/reduce_scatter | solution.py:164
  372.6 18.6 %all-gather.11.cloned.1.call-done = bf16[1024,2,512]{2,0,1:T(8,128)(2,1)} async-done(((bf16[256,2,512]{2,0,1:T(8,128)(2,1)}), bf16[1024,2,512]{2,0,1:T(8,128)(2,1)}) %all-gather.11.cloned.1.call-update) | async-done | bytes 2097168 | tf_op jit(solution)/shard_map/all_gather | solution.py:175
  395.0 4.5 fusion.173
  399.6 23.3 %fusion.17 = f32[2,2,64,512]{3,2,1,0:T(8,128)} fusion(bf16[1024,2,2,64]{0,3,2,1:T(8,128)(2,1)S(1)} %copy-done.33, f32[2,2,512,1024]{3,2,1,0:T(8,128)} %fusion.173, f32[2,2,512,1024]{3,2,1,0:T(8,128)} %copy-done.6, f32[2,2,512]{2,1,0:T(2,128)S(1)} %copy-done.49, pred[2,512,1024]{2,1,0:T(8,128)(4,1)} %copy-done.16), kind=kOutput, calls=%fused_computation.23 | convolution fusion | flops 291507200 | bytes 18882560 | tf_op jit(solution)/shard_map/shqk,kshe->qshe/dot_general | solution.py:200
  422.8 19.2 %fusion.14 = f32[2,2,64,1024]{3,2,1,0:T(8,128)} fusion(f32[2,2,512,1024]{3,2,1,0:T(8,128)} %fusion.173, f32[2,2,512,1024]{3,2,1,0:T(8,128)} %copy-done.6, f32[2,2,512]{2,1,0:T(2,128)S(1)} %copy-done.49, pred[2,512,1024]{2,1,0:T(8,128)(4,1)} %copy-done.16, bf16[1024,2,2,64]{0,3,2,1:T(8,128)(2,1)} %copy-done.31), kind=kOutput, calls=%fused_computation.22 | convolution fusion | flops 291507200 | bytes 36978688 | tf_op jit(solution)/shard_map/shqk,qshe->kshe/dot_general | solution.py:202
  442.0 4.5 fusion.174
  446.6 5.0 fusion.56
  451.6 3.5 fusion.91
  458.1 18.4 %fusion.24 = f32[2,2,64,512]{3,2,1,0:T(8,128)} fusion(bf16[1024,2,2,64]{0,3,2,1:T(8,128)(2,1)} %copy-done.32, f32[2,2,512,1024]{3,2,1,0:T(8,128)} %fusion.174, f32[2,2,512,1024]{3,2,1,0:T(8,128)} %copy-done.5, f32[2,2,512]{2,1,0:T(2,128)S(1)} %copy-done.48, pred[2,512,1024]{2,1,0:T(8,128)(4,1)} %copy-done.14), kind=kOutput, calls=%fused_computation.26 | convolution fusion | flops 291507200 | bytes 18882560 | tf_op jit(solution)/shard_map/shqk,kshe->qshe/dot_general | solution.py:200
  476.6 20.5 %maximum_multiply_fusion.3 = (f32[1024,2,2,64]{0,3,2,1:T(8,128)}, f32[1024,2,2,64]{0,3,2,1:T(8,128)}, f32[1024,2,2,64]{0,3,2,1:T(8,128)}) fusion(f32[512,2,2,64]{0,3,2,1:T(8,128)} %bitcast.124, f32[512,2,2,64]{0,3,2,1:T(8,128)S(1)} %bitcast.123, f32[1024,64]{0,1:T(8,128)S(1)} %copy-done.25, f32[2,2,64,1024]{3,2,1,0:T(8,128)} %fusion.14, ...), kind=kOutput, calls=%fused_computation.107 | convolution fusion | flops 292555776 | bytes 41435136 | tf_op jit(solution)/shard_map/shqk,qshe->kshe/dot_general | solution.py:202
  515.3 4.6 convolution_bitcast_fusion
  520.0 4.7 convolution_bitcast_fusion.2
  525.0 4.5 convolution_bitcast_fusion.1
  536.7 56.9 %all-reduce.5.cloned.1.call-done = f32[3,512,128]{2,0,1:T(4,128)} async-done(((f32[3,512,128]{2,0,1:T(4,128)}), f32[3,512,128]{2,0,1:T(4,128)}) %all-reduce.5.cloned.1.call-update) | async-done | bytes 786448
  595.2 45.1 %reduce-scatter.14.cloned.1.call-done = f32[256,2,512]{2,0,1:T(8,128)} async-done(((f32[1024,2,512]{2,0,1:T(8,128)}), f32[256,2,512]{2,0,1:T(8,128)}) %reduce-scatter.14.cloned.1.call-update) | async-done | bytes 1048592 | tf_op jit(solution)/shard_map/reduce_scatter | solution.py:225
  644.0 40.0 %all-reduce.2 = (f32[]{:T(128)}, f32[512]{0:T(512)}, f32[512]{0:T(512)}, f32[512]{0:T(512)}, f32[512]{0:T(512)}) all-reduce(f32[]{:T(128)} %fusion.98, f32[512]{0:T(512)S(1)} %get-tuple-element.68, f32[512]{0:T(512)S(1)} %get-tuple-element.73, f32[512]{0:T(512)S(1)} %copy-done.50, ...), channel_id=1, replica_groups=mesh['dp'=8,'tensor'=4] {'dp','tensor'}, use_global_device_ids=true, to_apply=%region_11.12 | all-reduce | flops 2049 | bytes 16392 | tf_op jit(solution)/shard_map/psum | solution.py:240
  688.3 20.3 %reduce-scatter.18.cloned.1.call-done = f32[64,512]{1,0:T(8,128)} async-done(((f32[512,512]{1,0:T(8,128)}), f32[64,512]{1,0:T(8,128)}) %reduce-scatter.18.cloned.1.call-update) | async-done | bytes 131088 | tf_op jit(solution)/shard_map/reduce_scatter | solution.py:237
  708.5 67.1 %reduce-scatter.20.cloned.1.call-done = f32[512,64]{0,1:T(8,128)} async-done(((f32[512,512]{0,1:T(8,128)}), f32[512,64]{0,1:T(8,128)}) %reduce-scatter.20.cloned.1.call-update) | async-done | bytes 131088 | tf_op jit(solution)/shard_map/reduce_scatter | solution.py:238
  775.7 64.8 %reduce-scatter.16.cloned.1.call-done = f32[128,64]{0,1:T(8,128)} async-done(((f32[128,512]{0,1:T(8,128)}), f32[128,64]{0,1:T(8,128)}) %reduce-scatter.16.cloned.1.call-update) | async-done | bytes 32784 | tf_op jit(solution)/shard_map/reduce_scatter | solution.py:236
  (226 shorter events, 93.4 us)
Async XLA Ops:
  7.2 39.6 %copy-start.35 = (bf16[3,64,128]{2,1,0:T(8,128)(2,1)S(1)}, bf16[3,64,128]{2,1,0:T(8,128)(2,1)}, u32[]{:S(2)}) copy-start(bf16[3,64,128]{2,1,0:T(8,128)(2,1)} %param.13) | copy-start | bytes 147460
  7.2 70.7 %copy-start.52 = (s32[2]{0:T(128)S(1)}, s32[2]{0:T(128)}, u32[]{:S(2)}) copy-start(s32[2]{0:T(128)} %param.21) | copy-start | bytes 28
  7.2 72.2 %all-gather.5.cloned.1.call-start = ((), (), s32[]{:S(2)}) async-start(), calls=%async_computation.7 | async-start | bytes 2621440 | tf_op jit(solution)/shard_map/all_gather | solution.py:77
  10.5 72.2 %copy-start.43 = (f32[256,2]{0,1:T(2,128)}, f32[256,2]{0,1:T(2,128)S(1)}, u32[]{:S(2)}) copy-start(f32[256,2]{0,1:T(2,128)S(1)} %multiply_reduce_fusion.7) | copy-start | bytes 6148
  10.5 72.2 %copy-start.39 = (f32[256,2]{0,1:T(2,128)}, f32[256,2]{0,1:T(2,128)S(1)}, u32[]{:S(2)}) copy-start(f32[256,2]{0,1:T(2,128)S(1)} %fusion.130) | copy-start | bytes 6148
  12.9 135.7 %reduce-scatter.8.cloned.1.call-start = ((), (), s32[]{:S(2)}) async-start(), calls=%async_computation.8 | async-start | bytes 5242880 | tf_op jit(solution)/shard_map/reduce_scatter | solution.py:116
  79.3 16.9 %copy-start.16 = (pred[2,512,1024]{2,1,0:T(8,128)(4,1)}, pred[2,512,1024]{2,1,0:T(8,128)(4,1)S(1)}, u32[]{:S(2)}) copy-start(pred[2,512,1024]{2,1,0:T(8,128)(4,1)S(1)} %get-tuple-element.107) | copy-start | bytes 3145732
  100.1 48.5 %copy-start = (f32[256,2,512]{2,1,0:T(2,128)S(1)}, f32[256,2,512]{2,1,0:T(2,128)}, u32[]{:S(2)}) copy-start(f32[256,2,512]{2,1,0:T(2,128)} %param.12) | copy-start | bytes 3145732
  102.8 47.7 %copy-start.46 = (f32[512]{0:T(512)S(1)}, f32[512]{0:T(512)}, u32[]{:S(2)}) copy-start(f32[512]{0:T(512)} %param.19) | copy-start | bytes 6148
  102.8 47.7 %copy-start.57 = (f32[512]{0:T(512)S(1)}, f32[512]{0:T(512)}, u32[]{:S(2)}) copy-start(f32[512]{0:T(512)} %param.20) | copy-start | bytes 6148
  102.8 48.8 %copy-start.34 = (bf16[64,512]{1,0:T(8,128)(2,1)S(1)}, bf16[64,512]{1,0:T(8,128)(2,1)}, u32[]{:S(2)}) copy-start(bf16[64,512]{1,0:T(8,128)(2,1)} %param.15) | copy-start | bytes 196612
  102.9 112.1 %all-gather.7.cloned.1.call-start = ((), (), s32[]{:S(2)}) async-start(), calls=%async_computation.9 | async-start | bytes 2621440 | tf_op jit(solution)/shard_map/all_gather | solution.py:127
  151.6 128.0 %reduce-scatter.10.cloned.1.call-start = ((), (), s32[]{:S(2)}) async-start(), calls=%async_computation.10 | async-start | bytes 5242880 | tf_op jit(solution)/shard_map/reduce_scatter | solution.py:136
  183.3 36.1 %copy-start.21 = (bf16[512,512]{1,0:T(8,128)(2,1)}, bf16[512,512]{1,0:T(8,128)(2,1)S(1)}, u32[]{:S(2)}) copy-start(bf16[512,512]{1,0:T(8,128)(2,1)S(1)} %all_gather.34) | copy-start | bytes 1572868
  234.8 71.0 %all-gather.9.cloned.1.call-start = ((), (), s32[]{:S(2)}) async-start(), calls=%async_computation.11 | async-start | bytes 2621440 | tf_op jit(solution)/shard_map/all_gather | solution.py:149
  283.0 78.7 %reduce-scatter.12.cloned.1.call-start = ((), (), s32[]{:S(2)}) async-start(), calls=%async_computation.12 | async-start | bytes 5242880 | tf_op jit(solution)/shard_map/reduce_scatter | solution.py:164
  317.0 74.1 %all-gather.11.cloned.1.call-start = ((), (), s32[]{:S(2)}) async-start(), calls=%async_computation.13 | async-start | bytes 2621440 | tf_op jit(solution)/shard_map/all_gather | solution.py:175
  367.5 27.6 %copy-start.11 = (bf16[1,1024,2,128]{1,3,0,2:T(8,128)(2,1)S(1)}, bf16[1,1024,2,128]{1,3,0,2:T(8,128)(2,1)}, u32[]{:S(2)}) copy-start(bf16[1,1024,2,128]{1,3,0,2:T(8,128)(2,1)} %copy-done.10) | copy-start | bytes 1572868
  368.4 225.2 %all-reduce.5.cloned.1.call-start = ((), (), s32[]{:S(2)}) async-start(), calls=%async_computation.18 | async-start | bytes 2097152
  422.8 19.2 %copy-start.28 = (bf16[512,2,128]{0,2,1:T(8,128)(2,1)S(1)}, bf16[512,2,128]{0,2,1:T(8,128)(2,1)}, u32[]{:S(2)}) copy-start(bf16[512,2,128]{0,2,1:T(8,128)(2,1)} %get-tuple-element.100) | copy-start | bytes 786436
  458.1 18.4 %copy-start.25 = (f32[1024,64]{0,1:T(8,128)S(1)}, f32[1024,64]{0,1:T(8,128)}, u32[]{:S(2)}) copy-start(f32[1024,64]{0,1:T(8,128)} %pad_maximum_fusion.6) | copy-start | bytes 786436
  515.2 125.1 %reduce-scatter.14.cloned.1.call-start = ((), (), s32[]{:S(2)}) async-start(), calls=%async_computation.14 | async-start | bytes 5242880 | tf_op jit(solution)/shard_map/reduce_scatter | solution.py:225
  519.9 188.6 %reduce-scatter.18.cloned.1.call-start = ((), (), s32[]{:S(2)}) async-start(), calls=%async_computation.16 | async-start | bytes 1179648 | tf_op jit(solution)/shard_map/reduce_scatter | solution.py:237
  524.7 250.9 %reduce-scatter.20.cloned.1.call-start = ((), (), s32[]{:S(2)}) async-start(), calls=%async_computation.17 | async-start | bytes 1179648 | tf_op jit(solution)/shard_map/reduce_scatter | solution.py:238
  529.5 110.9 %copy-start.41 = (f32[512]{0:T(512)S(1)}, f32[512]{0:T(512)}, u32[]{:S(2)}) copy-start(f32[512]{0:T(512)} %param.17) | copy-start | bytes 6148
  529.5 310.9 %reduce-scatter.16.cloned.1.call-start = ((), (), s32[]{:S(2)}) async-start(), calls=%async_computation.15 | async-start | bytes 294912 | tf_op jit(solution)/shard_map/reduce_scatter | solution.py:236
  532.8 109.3 %copy-start.44 = (f32[256,2]{0,1:T(2,128)S(1)}, f32[256,2]{0,1:T(2,128)}, u32[]{:S(2)}) copy-start(f32[256,2]{0,1:T(2,128)} %copy-done.43) | copy-start | bytes 6148
  532.8 109.4 %copy-start.40 = (f32[256,2]{0,1:T(2,128)S(1)}, f32[256,2]{0,1:T(2,128)}, u32[]{:S(2)}) copy-start(f32[256,2]{0,1:T(2,128)} %copy-done.39) | copy-start | bytes 6148
  535.0 109.0 %copy-start.50 = (f32[512]{0:T(512)S(1)}, f32[512]{0:T(512)}, u32[]{:S(2)}) copy-start(f32[512]{0:T(512)} %get-tuple-element.70) | copy-start | bytes 6148
  535.0 109.0 %copy-start.51 = (f32[512]{0:T(512)S(1)}, f32[512]{0:T(512)}, u32[]{:S(2)}) copy-start(f32[512]{0:T(512)} %get-tuple-element.72) | copy-start | bytes 6148
  535.0 149.0 %copy-start.2 = (f32[256,2,512]{2,0,1:T(8,128)S(1)}, f32[256,2,512]{2,0,1:T(8,128)}, u32[]{:S(2)}) copy-start(f32[256,2,512]{2,0,1:T(8,128)} %get-tuple-element.83) | copy-start | bytes 3145732
  640.4 43.7 %copy-start.3 = (f32[256,2,512]{2,0,1:T(8,128)S(1)}, f32[256,2,512]{2,0,1:T(8,128)}, u32[]{:S(2)}) copy-start(f32[256,2,512]{2,0,1:T(8,128)} %reduce-scatter.14.cloned.1.call-done) | copy-start | bytes 3145732
  (41 other events, 202.4 us)
Sparse Core Ops, SparseCore 0:
  13.0 25.2 all-gather.4
  103.0 45.6 reduce-scatter.7
  151.7 22.5 all-gather.6
  234.9 44.5 reduce-scatter.9
  283.2 22.5 all-gather.8
  317.2 44.5 reduce-scatter.11
  368.5 22.5 all-gather.10
  515.4 78.2 all-reduce.4
  596.2 44.1 reduce-scatter.13
  644.2 64.2 reduce-scatter.17
  712.5 63.1 reduce-scatter.19
  779.4 60.9 reduce-scatter.15
